TPU v7x, 128 devices: a whole 4x4x4 slice. The times are simulated.
128 devices in a mesh: rep: 8 (over z, y_lo), fsdp: 16 (over y_hi, x, core).
Axes of the slice: x: 4, y: 4 (y_hi: 2, y_lo: 2; y = y_hi * 2 + y_lo), z: 4, core: 2. Of those that a mesh axis runs over, the one named last changes fastest.
Arguments:
- tokens: bfloat16 [65536, 2048], P(('rep', 'fsdp')), may hold values from -6 to 6
- norm_gain: float32 [2048], replicated, may hold values from 0.5 to 1.5
- outer_params: float32 [2, 2048, 4096], P(None, 'fsdp'), may hold values from -6 to 6
- momentum: float32 [2, 2048, 4096], P(None, 'fsdp'), may hold values from -6 to 6
- deltas: bfloat16 [8, 2, 2048, 4096], P('rep', None, 'fsdp'), may hold values from -6 to 6
Outputs:
- new_params: float32 [2, 2048, 4096], P(None, 'fsdp')
- new_momentum: float32 [2, 2048, 4096], P(None, 'fsdp')
- hidden: bfloat16 [65536, 4096], P(('rep', 'fsdp'))
All inputs are finite; a program needn't handle non-finite values.
Results may differ from a plain program's by a relative error of at most 0.01.
Values may be sent and summed in bfloat16 or wider, within the bound.
No kernel may reach another device: no remote copies, remote signals or barrier semaphores. Data moves between devices by JAX's collectives and lax.ppermute only.
A program may use at most 192 MiB of HBM per device.

v0:
```python
import math

import jax
import jax.numpy as jnp
from jax import lax
from jax.sharding import PartitionSpec as P

EPS = 1e-05
MU = 0.9
RATE = 0.7


def advance(params, moment, summed, groups):
    outer_grad = summed * (1.0 / groups)
    moment_next = MU * moment + outer_grad
    params_next = params - RATE * (outer_grad + MU * moment_next)
    return (params_next, moment_next)


def body(tokens, norm_gain, outer_params, momentum, deltas):
    groups = lax.axis_size("rep")
    own_delta = deltas[0].astype(jnp.float32)
    summed = lax.psum(own_delta.astype(jnp.bfloat16), "rep").astype(jnp.float32)
    new_params, new_momentum = advance(outer_params, momentum, summed, groups)
    weights = new_params.astype(jnp.bfloat16)
    values = tokens.astype(jnp.float32)
    scale_rows = lax.rsqrt(jnp.mean(values * values, axis=-1, keepdims=True) + EPS)
    normed = (values * scale_rows * norm_gain).astype(jnp.bfloat16)
    factor = 1.0 / math.sqrt(normed.shape[1])
    results = []
    for which in range(2):
        results.append(
            jnp.dot(
                normed,
                lax.all_gather(weights[which], "fsdp", axis=0, tiled=True),
                preferred_element_type=jnp.float32,
            )
        )
    gate, up = (results[0], results[1])
    hidden = (jax.nn.silu(gate * factor) * (up * factor)).astype(jnp.bfloat16)
    return (new_params, new_momentum, hidden)


def solution(mesh):
    in_specs = (
        P(("rep", "fsdp"), None),
        P(),
        P(None, "fsdp", None),
        P(None, "fsdp", None),
        P("rep", None, "fsdp", None),
    )
    out_specs = (P(None, "fsdp", None), P(None, "fsdp", None), P(("rep", "fsdp"), None))
    return jax.shard_map(body, mesh=mesh, in_specs=in_specs, out_specs=out_specs, check_vma=False)
```

profile of v0, /device:TPU:1, one launch (start us, length us, event | category | flops | bytes accessed | tf_op | source)
XLA Modules:
  0.0 376.3 jit_solution(11234318730406531627)
XLA Ops:
  7.2 0.0 all-reduce.2.cloned.1.call-start
  7.2 0.7 all-reduce.2.cloned.1.call-update
  7.9 0.0 all-gather.7.cloned.1.call-start
  7.9 109.9 %all-reduce.2.cloned.1.call-done = bf16[2,128,4096]{2,1,0:T(8,128)(2,1)} async-done(((bf16[2,128,4096]{2,1,0:T(8,128)(2,1)}), bf16[2,128,4096]{2,1,0:T(8,128)(2,1)}) %all-reduce.2.cloned.1.call-update) | async-done | bytes 2097168 | tf_op jit(solution)/shard_map/psum | solution.py:23
  117.9 9.4 %fusion.11 = (bf16[2,128,4096]{2,1,0:T(8,128)(2,1)S(1)}, f32[2,128,4096]{2,1,0:T(8,128)}, f32[2,128,4096]{2,1,0:T(8,128)}) fusion(f32[2,128,4096]{2,1,0:T(8,128)} %param.7, bf16[2,128,4096]{2,1,0:T(8,128)(2,1)} %all-reduce.2.cloned.1.call-done, f32[2,128,4096]{2,1,0:T(8,128)} %param.8), kind=kLoop, calls=%fused_computation.14 | loop fusion | flops 9437184 | bytes 20971520 | tf_op jit(solution)/shard_map/convert_element_type | solution.py:25
  127.3 0.0 copy-start
  127.3 0.0 copy-start.1
  127.3 1.5 fusion.12
  128.7 0.0 all-gather.7.cloned.1.call-update
  128.7 0.0 all-gather.5.cloned.1.call-start
  128.8 0.7 all-gather.5.cloned.1.call-update
  129.5 0.1 copy-done
  129.6 0.5 fusion.6
  130.1 108.7 %all-gather.7.cloned.1.call-done = bf16[1,2048,4096]{2,1,0:T(8,128)(2,1)} async-done(((bf16[1,128,4096]{2,1,0:T(8,128)(2,1)}), bf16[1,2048,4096]{2,1,0:T(8,128)(2,1)}) %all-gather.7.cloned.1.call-update) | async-done | bytes 16777232 | tf_op jit(solution)/shard_map/all_gather | solution.py:35
  238.8 0.0 copy-done.1
  238.8 14.4 %fusion = f32[512,4096]{1,0:T(8,128)} fusion(bf16[1,2048,4096]{2,1,0:T(8,128)(2,1)} %all-gather.7.cloned.1.call-done, bf16[512,2048]{1,0:T(8,128)(2,1)S(1)} %copy-done, f32[2048]{0:T(1024)S(1)} %copy-done.1, f32[512]{0:T(512)S(1)} %add_rsqrt_fusion), kind=kOutput, calls=%fused_computation | convolution fusion | flops 8594128896 | bytes 27273216 | tf_op jit(solution)/shard_map/dot_general | solution.py:33
  253.2 96.1 %all-gather.5.cloned.1.call-done = bf16[1,2048,4096]{2,1,0:T(8,128)(2,1)} async-done(((bf16[1,128,4096]{2,1,0:T(8,128)(2,1)}), bf16[1,2048,4096]{2,1,0:T(8,128)(2,1)}) %all-gather.5.cloned.1.call-update) | async-done | bytes 16777232 | tf_op jit(solution)/shard_map/all_gather | solution.py:35
  349.3 20.5 %multiply_convert_fusion = bf16[512,4096]{1,0:T(8,128)(2,1)} fusion(f32[512,4096]{1,0:T(8,128)} %fusion, bf16[1,2048,4096]{2,1,0:T(8,128)(2,1)} %all-gather.5.cloned.1.call-done, bf16[512,2048]{1,0:T(8,128)(2,1)S(1)} %copy-done, f32[2048]{0:T(1024)S(1)} %copy-done.1, f32[512]{0:T(512)S(1)} %add_rsqrt_fusion), kind=kOutput, calls=%fused_computation.4 | convolution fusion | flops 8610906112 | bytes 31467520 | tf_op jit(solution)/shard_map/dot_general | solution.py:33
  (1 shorter events, 0.0 us)
Async XLA Ops:
  7.2 110.7 %all-reduce.2.cloned.1.call-start = ((), (), s32[]{:S(2)}) async-start(), calls=%async_computation | async-start | bytes 4194304 | tf_op jit(solution)/shard_map/psum | solution.py:23
  7.9 230.9 %all-gather.7.cloned.1.call-start = ((), (), s32[]{:S(2)}) async-start(), calls=%async_computation.2 | async-start | bytes 17825792 | tf_op jit(solution)/shard_map/all_gather | solution.py:35
  127.3 2.3 copy-start
  127.3 111.6 %copy-start.1 = (f32[2048]{0:T(1024)S(1)}, f32[2048]{0:T(1024)}, u32[]{:S(2)}) copy-start(f32[2048]{0:T(1024)} %param.6) | copy-start | bytes 24580
  128.7 220.6 %all-gather.5.cloned.1.call-start = ((), (), s32[]{:S(2)}) async-start(), calls=%async_computation.1 | async-start | bytes 17825792 | tf_op jit(solution)/shard_map/all_gather | solution.py:35
Sparse Core Ops, SparseCore 0:
  10.5 107.3 all-reduce.1
  128.9 109.9 all-gather.6
  241.8 107.4 all-gather.4
where the time goes:
time: 376 us
  waiting for transfers between devices  316 us (84%)
  matrix products  34.9 us (9%)
  between operations  13.7 us (4%)
  other arithmetic  9.89 us (3%)
    all_gather x2, waiting for transfers between devices, body(): lax.all_gather(weights[which], 'fsdp', axis=0, tiled=True)  205 us
    psum x1, waiting for transfers between devices, body(): summed = lax.psum(own_delta.astype(jnp.bfloat16), 'rep').astype(jnp.float32)  110 us
    dot_general x2, matrix products, body(): jnp.dot(normed, lax.all_gather(weights[which], 'fsdp', axis=0, tiled=True...  34.9 us
    convert_element_type x1, other arithmetic, body(): weights = new_params.astype(jnp.bfloat16)  9.4 us
  transfers between devices with their start and end apart: 3, of which 3 were waited for; matrix products, arithmetic and copies ran while one was open for 4% of the time, Pallas kernels for 0%

commit v1 on v0

v1 whole, which is shorter than its diff:
```python
import math

import jax
import jax.numpy as jnp
from jax import lax
from jax.experimental import pallas as pl
from jax.experimental.pallas import tpu as pltpu
from jax.sharding import PartitionSpec as P


EPS = 1e-05
MU = 0.9
RATE = 0.7

AXES = ("rep", "fsdp")
BLK = 256


def permute(value, target):
    pairs = []
    for z in range(4):
        for yl in range(2):
            for yh in range(2):
                for x in range(4):
                    for c in range(2):
                        z2, y2, x2, c2 = target(z, 2 * yh + yl, x, c)
                        z2, y2, x2 = z2 % 4, y2 % 4, x2 % 4
                        here = (((z * 2 + yl) * 2 + yh) * 4 + x) * 2 + c
                        there = (((z2 * 2 + y2 % 2) * 2 + y2 // 2) * 4 + x2) * 2 + c2
                        pairs.append((here, there))
    return lax.ppermute(value, AXES, pairs)


def decode(place):
    code = place[0]
    c = code % 2
    x = (code // 2) % 4
    yh = (code // 8) % 2
    yl = (code // 16) % 2
    z = code // 32
    return z, yl, yh, x, c


def column_block(z, yl, c):
    return (((z % 2) * 2 + c) * 2 + z // 2) * 2 + yl


ANY = pl.BlockSpec(memory_space=pl.ANY)
SMEM = pl.BlockSpec(memory_space=pltpu.SMEM)
SHIFTS = [(dz, dy) for dz in range(4) for dy in range(2)]


def pack_kernel(place, deltas, *refs):
    outs, held, sems = refs[:8], refs[8], refs[9]
    z, yl, _, _, _ = decode(place)
    loads, stores = [], []
    for k, (dz, dy) in enumerate(SHIFTS):
        for c in range(2):
            block = column_block((z + dz) % 4, (yl + dy) % 2, c)
            columns = pl.ds(pl.multiple_of(block * BLK, BLK), BLK)
            loads.append(pltpu.make_async_copy(deltas.at[:, :, columns], held.at[k, c], sems.at[2 * k + c]))
        stores.append(pltpu.make_async_copy(held.at[k], outs[k], sems.at[16 + k]))
    order = list(range(1, 8)) + [0]
    for k in order:
        loads[2 * k].start()
        loads[2 * k + 1].start()
    for k in order:
        loads[2 * k].wait()
        loads[2 * k + 1].wait()
        stores[k].start()
    for store in stores:
        store.wait()


def pack(place, deltas):
    rows = deltas.shape[1]
    return pl.pallas_call(
        pack_kernel,
        in_specs=[SMEM, ANY],
        out_specs=[ANY] * 8,
        out_shape=[jax.ShapeDtypeStruct((2, 2, rows, BLK), deltas.dtype)] * 8,
        scratch_shapes=[pltpu.VMEM((8, 2, 2, rows, BLK), deltas.dtype), pltpu.SemaphoreType.DMA((24,))],
        name="pack",
    )(place, deltas)


def advance(params, moment, outer_grad):
    moment_next = MU * moment + outer_grad
    return params - RATE * (outer_grad + MU * moment_next), moment_next


def reduce_kernel(place, *refs):
    parts, outer, moment, sums, keep, give = refs[:8], refs[8], refs[9], refs[10], refs[11], refs[12]
    total = parts[0][0].astype(jnp.float32)
    for part in parts[1:]:
        total = total + part[0].astype(jnp.float32)
    rounded = total.astype(jnp.bfloat16)
    sums[0] = rounded
    params, _ = advance(outer[...], moment[...], rounded.astype(jnp.float32) * 0.125)
    weights = params.astype(jnp.bfloat16)

    @pl.when(pl.program_id(0) == 0)
    def _():
        give[:, :BLK] = weights[0]
        give[:, BLK:] = weights[1]

    @pl.when(pl.program_id(0) == 1)
    def _():
        keep[:, :BLK] = weights[0]
        keep[:, BLK:] = weights[1]


def reduce_update(place, parts, outer, moment):
    rows = outer.shape[1]

    def core(j, place):
        return 1 - (place[0] + j) % 2

    def columns(j, place):
        z, yl, _, _, _ = decode(place)
        return (0, 0, column_block(z, yl, core(j, place)))

    piece = pl.BlockSpec((1, 2, rows, BLK), lambda j, place: (core(j, place), 0, 0, 0))
    state = pl.BlockSpec((2, rows, BLK), columns)
    whole = pl.BlockSpec((rows, 2 * BLK), lambda j, place: (0, 0))
    shape = jax.ShapeDtypeStruct((rows, 2 * BLK), jnp.bfloat16)
    return pl.pallas_call(
        reduce_kernel,
        grid_spec=pltpu.PrefetchScalarGridSpec(
            num_scalar_prefetch=1,
            grid=(2,),
            in_specs=[piece] * 8 + [state, state],
            out_specs=[piece, whole, whole],
        ),
        out_shape=[jax.ShapeDtypeStruct((2, 2, rows, BLK), jnp.bfloat16), shape, shape],
        name="reduce_update",
    )(place, *parts, outer, moment)


def finish_kernel(place, sums, outer, moment, params_out, moment_out):
    _, yl, _, _, _ = decode(place)
    low = jnp.where(yl == 0, sums[0, 0, 0], sums[0, 1, 0]).astype(jnp.float32)
    high = jnp.where(yl == 0, sums[0, 1, 0], sums[0, 0, 0]).astype(jnp.float32)
    for half, total in enumerate((low, high)):
        at = (slice(None), slice(None), slice(half * BLK, (half + 1) * BLK))
        params_out[at], moment_out[at] = advance(outer[at], moment[at], total * 0.125)


def finish(place, sums, outer, moment):
    rows = outer.shape[1]

    def columns(i, c, place):
        z = (decode(place)[0] + i) % 4
        return (0, 0, ((z % 2) * 2 + c) * 2 + z // 2)

    state = pl.BlockSpec((2, rows, 2 * BLK), columns)
    return pl.pallas_call(
        finish_kernel,
        grid_spec=pltpu.PrefetchScalarGridSpec(
            num_scalar_prefetch=1,
            grid=(4, 2),
            in_specs=[pl.BlockSpec((1, 2, 1, 2, rows, BLK), lambda i, c, place: (i, 0, c, 0, 0, 0)), state, state],
            out_specs=[state, state],
        ),
        out_shape=[jax.ShapeDtypeStruct(outer.shape, jnp.float32)] * 2,
        name="finish",
    )(place, sums, outer, moment)


def project_kernel(factor, count, place, *refs):
    tokens, first, second = refs[:count], refs[count : count + 4], refs[count + 4 : count + 8]
    outs, weights, sems = refs[count + 8 : 2 * count + 8], refs[-2], refs[-1]
    z, yl, yh, x, c = decode(place)
    y = 2 * yh + yl
    copies = [[], [], [], []]
    for i in range(4):
        for j in range(4):
            for k in range(2):
                core = (c + k) % 2
                for group in range(2):
                    dx, dy = (i, j) if group == 0 else (j, i)
                    row = (((y + dy) % 4) // 2) * 8 + ((x + dx) % 4) * 2 + core
                    block = 2 * group + dy % 2
                    source = (first, second)[group][i].at[j, k]
                    target = weights.at[block, pl.ds(pl.multiple_of(row * 128, 128), 128), :]
                    copies[block].append(pltpu.make_async_copy(source, target, sems.at[block, len(copies[block])]))
    for group in copies:
        for copy in group:
            copy.start()
    for block in range(4):
        for copy in copies[block]:
            copy.wait()
        zh = (z // 2 + block // 2) % 2
        at = zh * 2 + (yl + block) % 2
        for t in range(count):
            both = jnp.dot(tokens[t][...], weights[block], preferred_element_type=jnp.float32) * factor
            gate, up = both[:, :BLK], both[:, BLK:]
            hidden = (gate / (1.0 + jnp.exp(-gate)) * up).astype(jnp.bfloat16)
            outs[t][:, pl.ds(pl.multiple_of(at * BLK, BLK), BLK)] = hidden


def project(place, tokens, first, second):
    count, width = tokens[0].shape
    vmem = pl.BlockSpec(memory_space=pltpu.VMEM)
    return pl.pallas_call(
        lambda *refs: project_kernel(1.0 / math.sqrt(width), len(tokens), *refs),
        in_specs=[SMEM] + [vmem] * len(tokens) + [ANY] * 8,
        out_specs=[vmem] * len(tokens),
        out_shape=[jax.ShapeDtypeStruct((count, 4 * BLK), jnp.bfloat16)] * len(tokens),
        scratch_shapes=[pltpu.VMEM((4, width, 2 * BLK), jnp.bfloat16), pltpu.SemaphoreType.DMA((4, 16))],
        name="project",
    )(place, *tokens, *first, *second)


def fill_kernel(kinds, place, *refs):
    count = len(kinds)
    pieces, out, held, sems = refs[:count], refs[-3], refs[-2], refs[-1]
    z, _, _, _, c = decode(place)
    p = z % 2
    loads, stores = [], []
    for k, (same_p, same_c) in enumerate(kinds):
        block = 2 * (p if same_p else 1 - p) + (c if same_c else 1 - c)
        columns = pl.ds(pl.multiple_of(block * 4 * BLK, 4 * BLK), 4 * BLK)
        loads.append(pltpu.make_async_copy(pieces[k], held.at[k], sems.at[0, k]))
        stores.append(pltpu.make_async_copy(held.at[k], out.at[:, columns], sems.at[1, k]))
    for load in loads:
        load.start()
    for load, store in zip(loads, stores):
        load.wait()
        store.start()
    for store in stores:
        store.wait()


def fill(place, pieces, kinds, whole=None):
    count, width = pieces[0].shape
    given = [] if whole is None else [whole]
    return pl.pallas_call(
        lambda *refs: fill_kernel(kinds, *refs),
        in_specs=[SMEM] + [ANY] * (len(pieces) + len(given)),
        out_specs=ANY,
        out_shape=jax.ShapeDtypeStruct((count, 4 * width), pieces[0].dtype),
        input_output_aliases={1 + len(pieces): 0} if given else {},
        scratch_shapes=[
            pltpu.VMEM((len(pieces), count, width), pieces[0].dtype),
            pltpu.SemaphoreType.DMA((2, len(pieces))),
        ],
        name="fill",
    )(place, *pieces, *given)


def along_x(value):
    return [value] + [permute(value, lambda z, y, x, c, d=d: (z, y, x - d, c)) for d in (1, 2, 3)]


def along_y(value):
    return [value] + [permute(value, lambda z, y, x, c, d=d: (z, y - d, x, c)) for d in (1, 2, 3)]


def along_z(value):
    return [value] + [permute(value, lambda z, y, x, c, d=d: (z - d, y, x, c)) for d in (1, 2, 3)]


def other_core(value):
    return permute(value, lambda z, y, x, c: (z, y, x, 1 - c))


def after(value, *others):
    return lax.optimization_barrier((value,) + others)[0]


def step(tokens, norm_gain, outer_params, momentum, deltas):
    place = lax.axis_index(AXES).astype(jnp.int32).reshape(1)
    packed = pack(place, deltas[0])
    parts = [
        permute(piece, lambda z, y, x, c, dz=dz, dy=dy: (z + dz, y ^ dy, x, c))
        for piece, (dz, dy) in zip(packed[1:], SHIFTS[1:])
    ]

    values = tokens.astype(jnp.float32)
    scale_rows = lax.rsqrt(jnp.mean(values * values, axis=-1, keepdims=True) + EPS)
    normed = (values * scale_rows * norm_gain).astype(jnp.bfloat16)
    partner = other_core(after(normed, packed[0]))

    own_part = after(packed[0], normed)
    sums, keep, give = reduce_update(place, [own_part] + parts, outer_params, momentum)
    share = jnp.stack([keep, other_core(give)])

    far = permute(share, lambda z, y, x, c: (z + 2, y, x, c))
    first_own = jnp.stack(along_y(share))
    second_own = jnp.stack(along_x(far))
    first = along_x(first_own)
    second = along_y(second_own)

    pair = jnp.stack([sums, permute(after(sums, share), lambda z, y, x, c: (z, y ^ 1, x, c))])
    pair = after(pair, second_own)
    all_sums = jnp.stack(along_z(pair))
    new_params, new_momentum = finish(place, all_sums, outer_params, momentum)

    straight = permute(after(normed, second_own), lambda z, y, x, c: (z - 1 + 2 * c, y, x, c))
    crossed = other_core(after(straight, new_params))

    (straight,) = project(place, [straight], first, second)
    (crossed,) = project(place, [after(crossed, straight)], first, second)
    partner, own = project(place, [after(partner, crossed), normed], first, second)
    straight = permute(straight, lambda z, y, x, c: (z + 1 - 2 * c, y, x, c))
    crossed = permute(crossed, lambda z, y, x, c: (z - 1 + 2 * c, y, x, 1 - c))
    partner = other_core(partner)
    hidden = fill(place, [own, partner], [(True, True), (True, False)])
    hidden = fill(place, [straight], [(False, True)], hidden)
    hidden = fill(place, [crossed], [(False, False)], hidden)
    return (new_params, new_momentum, hidden)


def solution(mesh):
    in_specs = (
        P(("rep", "fsdp"), None),
        P(),
        P(None, "fsdp", None),
        P(None, "fsdp", None),
        P("rep", None, "fsdp", None),
    )
    out_specs = (P(None, "fsdp", None), P(None, "fsdp", None), P(("rep", "fsdp"), None))
    return jax.shard_map(step, mesh=mesh, in_specs=in_specs, out_specs=out_specs, check_vma=False)
```

time: 376 us -> 263 us (0.70)
  waiting for transfers between devices: 316 us -> 139 us
  Pallas kernels: 0 us -> 57.9 us
  starting transfers between devices: 0.12 us -> 55.2 us
  matrix products: 34.9 us -> 0 us
  between operations: 13.7 us -> 1.08 us
  other arithmetic: 9.89 us -> 5.2 us
    all_gather x2 -> x0, waiting for transfers between devices: 205 us -> none  [body(): lax.all_gather(weights[which], 'fsdp', axis=0, tiled=True)]
    ppermute x0 -> x31, waiting for transfers between devices: none -> 139 us  [permute(): return lax.ppermute(value, AXES, pairs)]
    psum x1 -> x0, waiting for transfers between devices: 110 us -> none  [body(): summed = lax.psum(own_delta.astype(jnp.bfloat16), 'rep').astype(jnp.float32)]
    pallas_call x0 -> x9, Pallas kernels: none -> 57.9 us  [the longest x3 35.5 us: project(): pl.pallas_call(lambda *refs: project_kernel(1.0 / math.sqrt(width), len(t...]
    ppermute x0 -> x31, starting transfers between devices: none -> 55.2 us  [permute(): return lax.ppermute(value, AXES, pairs)]
    dot_general x2 -> x0, matrix products: 34.9 us -> none  [body(): jnp.dot(normed, lax.all_gather(weights[which], 'fsdp', axis=0, tiled=True...]
    convert_element_type x1, other arithmetic: 9.4 us -> 1.88 us  [step(): normed = (values * scale_rows * norm_gain).astype(jnp.bfloat16)]
  transfers between devices with their start and end apart: 3 -> 31, of which waited for: 3 -> 15; matrix products, arithmetic and copies ran while one was open for 4% -> 2% of each run, Pallas kernels for 0% -> 13%
where the time goes in v1:
time: 263 us; the launch traced here: 262 us
  waiting for transfers between devices  139 us (53%)
  Pallas kernels  57.9 us (22%)
  starting transfers between devices  55.2 us (21%)
  other arithmetic  5.2 us (2%)
  local copies, waits for them, and re-layouts  3.8 us (1%)
    ppermute x31, waiting for transfers between devices, permute(): return lax.ppermute(value, AXES, pairs)  139 us
    ppermute x31, starting transfers between devices, permute(): return lax.ppermute(value, AXES, pairs)  55.2 us
    pallas_call x3, Pallas kernels, project(): pl.pallas_call(lambda *refs: project_kernel(1.0 / math.sqrt(width), len(t...  35.5 us
    pallas_call x1, Pallas kernels, finish(): pl.pallas_call(finish_kernel, grid_spec=pltpu.PrefetchScalarGridSpec(num_...  9.58 us
    pallas_call x3, Pallas kernels, fill(): pl.pallas_call(lambda *refs: fill_kernel(kinds, *refs), in_specs=[SMEM] +...  6.99 us
  transfers between devices with their start and end apart: 31, of which 15 were waited for; matrix products, arithmetic and copies ran while one was open for 2% of the time, Pallas kernels for 13%

profile of v1, /device:TPU:1, one launch (start us, length us, event | category | flops | bytes accessed | tf_op | source)
XLA Modules:
  0.0 262.3 jit_solution(10019238113785918694)
XLA Ops:
  0.7 2.7 %pack.1 = (bf16[2,2,128,256]{3,2,1,0:T(8,128)(2,1)}, bf16[2,2,128,256]{3,2,1,0:T(8,128)(2,1)}, bf16[2,2,128,256]{3,2,1,0:T(8,128)(2,1)}, bf16[2,2,128,256]{3,2,1...) custom-call(s32[1]{0:T(128)} %bitcast.place.refs_0_, ...), custom_call_target="tpu_custom_call" | custom-call | tf_op jit(solution)/shard_map/pack/pallas_call | solution.py:77
  3.4 2.2 collective-permute-start
  5.6 1.6 collective-permute-start.1
  7.2 1.5 collective-permute-start.2
  8.8 1.8 collective-permute-start.3
  10.6 2.2 collective-permute-start.4
  12.8 0.5 fusion
  13.3 0.0 copy-start.11
  13.3 2.2 collective-permute-start.5
  15.5 4.2 %collective-permute-done.1.refs_2_ = bf16[2,2,128,256]{3,2,1,0:T(8,128)(2,1)S(1)} collective-permute-done((bf16[2,2,128,256]{3,2,1,0:T(8,128)(2,1)}, bf16[2,2,128,256]{3,2,1,0:T(8,128)(2,1)S(1)}, u32[]{:S(2)}, u32[]{:S(2)}) %collective-permute-start.1) | collective-permute-done | bytes 262176 | tf_op jit(solution)/shard_map/ppermute | solution.py:31
  19.6 1.9 fusion.2.refs_2_
  21.5 11.6 %collective-permute-done.3.refs_4_ = bf16[2,2,128,256]{3,2,1,0:T(8,128)(2,1)S(1)} collective-permute-done((bf16[2,2,128,256]{3,2,1,0:T(8,128)(2,1)}, bf16[2,2,128,256]{3,2,1,0:T(8,128)(2,1)S(1)}, u32[]{:S(2)}, u32[]{:S(2)}) %collective-permute-start.3) | collective-permute-done | bytes 262176 | tf_op jit(solution)/shard_map/ppermute | solution.py:31
  33.2 0.7 copy-done.14
  33.8 0.1 copy-done.15
  33.9 3.1 %reduce_update.1 = (bf16[2,2,128,256]{3,2,1,0:T(8,128)(2,1)}, bf16[128,512]{1,0:T(8,128)(2,1)}, bf16[128,512]{1,0:T(8,128)(2,1)}) custom-call(s32[1]{0:T(128)} %bitcast.place.refs_0_, bf16[2,2,128,256]{3,2,1,0:T(8,128)(2,1)} %get-tuple-element.27.refs_0_, bf16[2,2,128,256]{3,2,1,0:T(8,128)(2,1)} %copy-done.11, bf16[2,2,128,256]{3,2,1,0:T(8,128)(2,1)} %copy-done.12, ...), custom_call_target="tpu_custom_call" | custom-call | tf_op jit(solution)/shard_map/reduce_update/pallas_call | solution.py:127
  37.0 1.9 collective-permute-start.7
  38.9 1.2 collective-permute-done.7
  40.1 0.9 fusion.3
  41.0 6.7 %collective-permute-start.9 = (bf16[2,128,512]{2,1,0:T(8,128)(2,1)S(1)}, bf16[2,128,512]{2,1,0:T(8,128)(2,1)S(1)}, u32[]{:S(2)}, u32[]{:S(2)}) collective-permute-start(bf16[2,128,512]{2,1,0:T(8,128)(2,1)S(1)} %get-tuple-element.50), channel_id=1, source_target_pairs={{0,64},{1,65},{2,66},{3,67},{4,68},{5,69},{6,70},{7,71},{8,72},{9,... | collective-permute-start | bytes 786440 | tf_op jit(solution)/shard_map/ppermute | solution.py:31
  47.8 6.3 %collective-permute-done.9 = bf16[2,128,512]{2,1,0:T(8,128)(2,1)S(1)} collective-permute-done((bf16[2,128,512]{2,1,0:T(8,128)(2,1)S(1)}, bf16[2,128,512]{2,1,0:T(8,128)(2,1)S(1)}, u32[]{:S(2)}, u32[]{:S(2)}) %collective-permute-start.9) | collective-permute-done | bytes 262176 | tf_op jit(solution)/shard_map/ppermute | solution.py:31
  54.1 1.2 collective-permute-start.12
  55.3 2.5 collective-permute-start.11
  57.8 1.2 collective-permute-start.10
  58.9 3.3 %collective-permute-done.12 = bf16[2,128,512]{2,1,0:T(8,128)(2,1)S(1)} collective-permute-done((bf16[2,128,512]{2,1,0:T(8,128)(2,1)S(1)}, bf16[2,128,512]{2,1,0:T(8,128)(2,1)S(1)}, u32[]{:S(2)}, u32[]{:S(2)}) %collective-permute-start.12) | collective-permute-done | bytes 262176 | tf_op jit(solution)/shard_map/ppermute | solution.py:31
  62.2 6.6 %collective-permute-done.11 = bf16[2,128,512]{2,1,0:T(8,128)(2,1)S(1)} collective-permute-done((bf16[2,128,512]{2,1,0:T(8,128)(2,1)S(1)}, bf16[2,128,512]{2,1,0:T(8,128)(2,1)S(1)}, u32[]{:S(2)}, u32[]{:S(2)}) %collective-permute-start.11) | collective-permute-done | bytes 262176 | tf_op jit(solution)/shard_map/ppermute | solution.py:31
  68.9 0.1 pad_maximum_fusion.1.refs_6_.refs_7_
  69.0 0.1 collective-permute-start.16
  69.1 0.6 collective-permute-start.8
  69.7 0.9 collective-permute-start.20
  70.6 2.6 collective-permute-start.19
  73.3 2.0 collective-permute-done.8
  75.2 0.1 pad_maximum_fusion.3
  75.3 2.5 collective-permute-start.15
  77.8 0.8 collective-permute-start.14
  78.7 2.2 collective-permute-start.13
  80.8 6.5 %collective-permute-done.19 = bf16[2,128,512]{2,1,0:T(8,128)(2,1)S(1)} collective-permute-done((bf16[2,128,512]{2,1,0:T(8,128)(2,1)S(1)}, bf16[2,128,512]{2,1,0:T(8,128)(2,1)S(1)}, u32[]{:S(2)}, u32[]{:S(2)}) %collective-permute-start.19) | collective-permute-done | bytes 262176 | tf_op jit(solution)/shard_map/ppermute | solution.py:31
  87.3 5.6 %collective-permute-done.18 = bf16[2,128,512]{2,1,0:T(8,128)(2,1)S(1)} collective-permute-done((bf16[2,128,512]{2,1,0:T(8,128)(2,1)S(1)}, bf16[2,128,512]{2,1,0:T(8,128)(2,1)S(1)}, u32[]{:S(2)}, u32[]{:S(2)}) %collective-permute-start.18) | collective-permute-done | bytes 262176 | tf_op jit(solution)/shard_map/ppermute | solution.py:31
  92.9 0.1 pad_maximum_fusion.2.refs_2_.refs_3_
  93.1 5.8 %collective-permute-start.21 = (bf16[4,2,128,512]{3,2,1,0:T(8,128)(2,1)S(1)}, bf16[4,2,128,512]{3,2,1,0:T(8,128)(2,1)S(1)}, u32[]{:S(2)}, u32[]{:S(2)}) collective-permute-start(bf16[4,2,128,512]{3,2,1,0:T(8,128)(2,1)S(1)} %pad_maximum_fusion.2.refs_2_.refs_3_), channel_id=1, source_target_pairs={{0,6},{1,7},{2,0},{3,1},{4,2},{5,3},{6,4},{7,5},{8,14},{9,15},{10,... | collective-permute-start | bytes 3145736 | tf_op jit(solution)/shard_map/ppermute | solution.py:31
  98.9 19.4 %collective-permute-done.15 = bf16[2,2,2,128,256]{4,3,2,1,0:T(8,128)(2,1)S(1)} collective-permute-done((bf16[2,2,2,128,256]{4,3,2,1,0:T(8,128)(2,1)S(1)}, bf16[2,2,2,128,256]{4,3,2,1,0:T(8,128)(2,1)S(1)}, u32[]{:S(2)}, u32[]{:S(2)}) %collective-permute-start.15) | collective-permute-done | bytes 524320 | tf_op jit(solution)/shard_map/ppermute | solution.py:31
  118.2 1.7 collective-permute-start.22
  120.0 2.0 collective-permute-start.23
  122.0 1.6 pad_maximum_fusion.sums
  123.6 9.6 %finish.1 = (f32[2,128,4096]{2,1,0:T(8,128)}, f32[2,128,4096]{2,1,0:T(8,128)}) custom-call(s32[1]{0:T(128)} %bitcast.place.refs_0_, bf16[4,2,2,2,128,256]{5,4,3,2,1,0:T(8,128)(2,1)} %pad_maximum_fusion.sums, f32[2,128,4096]{2,1,0:T(8,128)} %outer.1, f32[2,128,4096]{2,1,0:T(8,128)} %moment.1), custom_call_target="tpu_custom_call" | custom-call | tf_op jit(solution)/shard_map/finish/pallas_call | solution.py:157
  133.2 0.1 collective-permute-start.17
  133.3 0.5 collective-permute-start.29
  133.8 1.9 collective-permute-start.24
  135.7 4.3 %collective-permute-done.22.refs_4_.refs_5_ = bf16[4,2,128,512]{3,2,1,0:T(8,128)(2,1)} collective-permute-done((bf16[4,2,128,512]{3,2,1,0:T(8,128)(2,1)S(1)}, bf16[4,2,128,512]{3,2,1,0:T(8,128)(2,1)}, u32[]{:S(2)}, u32[]{:S(2)}) %collective-permute-start.22) | collective-permute-done | bytes 1048608 | tf_op jit(solution)/shard_map/ppermute | solution.py:31
  140.0 0.3 collective-permute-start.25
  140.3 10.9 %collective-permute-done.23.refs_5_.refs_6_ = bf16[4,2,128,512]{3,2,1,0:T(8,128)(2,1)} collective-permute-done((bf16[4,2,128,512]{3,2,1,0:T(8,128)(2,1)S(1)}, bf16[4,2,128,512]{3,2,1,0:T(8,128)(2,1)}, u32[]{:S(2)}, u32[]{:S(2)}) %collective-permute-start.23) | collective-permute-done | bytes 1048608 | tf_op jit(solution)/shard_map/ppermute | solution.py:31
  151.3 8.6 %collective-permute-done.25.refs_8_.refs_9_ = bf16[4,2,128,512]{3,2,1,0:T(8,128)(2,1)S(1)} collective-permute-done((bf16[4,2,128,512]{3,2,1,0:T(8,128)(2,1)S(1)}, bf16[4,2,128,512]{3,2,1,0:T(8,128)(2,1)S(1)}, u32[]{:S(2)}, u32[]{:S(2)}) %collective-permute-start.25) | collective-permute-done | bytes 1048608 | tf_op jit(solution)/shard_map/ppermute | solution.py:31
  159.9 1.0 copy-done.4
  160.9 28.2 %collective-permute-done.26.refs_9_.refs_10_ = bf16[4,2,128,512]{3,2,1,0:T(8,128)(2,1)S(1)} collective-permute-done((bf16[4,2,128,512]{3,2,1,0:T(8,128)(2,1)S(1)}, bf16[4,2,128,512]{3,2,1,0:T(8,128)(2,1)S(1)}, u32[]{:S(2)}, u32[]{:S(2)}) %collective-permute-start.26) | collective-permute-done | bytes 1048608 | tf_op jit(solution)/shard_map/ppermute | solution.py:31
  189.1 1.0 copy-done.5
  190.1 10.0 %project.3 = bf16[512,1024]{1,0:T(8,128)(2,1)} custom-call(s32[1]{0:T(128)} %bitcast.place.refs_0_, bf16[512,2048]{1,0:T(8,128)(2,1)} %collective-permute-done.16.refs_1_, bf16[4,2,128,512]{3,2,1,0:T(8,128)(2,1)} %copy-done.1, bf16[4,2,128,512]{3,2,1,0:T(8,128)(2,1)} %copy-done.2, bf16[4,2,128,512]{3,2,1,0:T(8,128)(2,1)} %collective-permute-done.22.refs_4_.refs_5_, ...), custom_call_target="tpu_custom_call" | custom-call | tf_op jit(solution)/shard_map/project/pallas_call | solution.py:205
  200.1 10.1 %project.4 = bf16[512,1024]{1,0:T(8,128)(2,1)} custom-call(s32[1]{0:T(128)} %bitcast.place.refs_0_, bf16[512,2048]{1,0:T(8,128)(2,1)} %collective-permute-done.17.refs_1_, bf16[4,2,128,512]{3,2,1,0:T(8,128)(2,1)} %copy-done.1, bf16[4,2,128,512]{3,2,1,0:T(8,128)(2,1)} %copy-done.2, bf16[4,2,128,512]{3,2,1,0:T(8,128)(2,1)} %collective-permute-done.22.refs_4_.refs_5_, ...), custom_call_target="tpu_custom_call" | custom-call | tf_op jit(solution)/shard_map/project/pallas_call | solution.py:205
  210.2 15.4 %project.5 = (bf16[512,1024]{1,0:T(8,128)(2,1)}, bf16[512,1024]{1,0:T(8,128)(2,1)}) custom-call(s32[1]{0:T(128)} %bitcast.place.refs_0_, bf16[512,2048]{1,0:T(8,128)(2,1)} %collective-permute-done.29.refs_1_, bf16[512,2048]{1,0:T(8,128)(2,1)} %fusion.2.refs_2_, bf16[4,2,128,512]{3,2,1,0:T(8,128)(2,1)} %copy-done.1, bf16[4,2,128,512]{3,2,1,0:T(8,128)(2,1)} %copy-done.2, ...), custom_call_target="tpu_custom_call" | custom-call | tf_op jit(solution)/shard_map/project/pallas_call | solution.py:205
  225.6 0.5 collective-permute-start.30
  226.1 7.6 %collective-permute-start.27 = (bf16[512,1024]{1,0:T(8,128)(2,1)S(1)}, bf16[512,1024]{1,0:T(8,128)(2,1)S(1)}, u32[]{:S(2)}, u32[]{:S(2)}) collective-permute-start(bf16[512,1024]{1,0:T(8,128)(2,1)S(1)} %copy-done.7), channel_id=1, source_target_pairs={{0,97},{1,32},{2,99},{3,34},{4,101},{5,36},{6,103},{7,38},{8,105},... | collective-permute-start | bytes 3145736 | tf_op jit(solution)/shard_map/ppermute | solution.py:31
  233.6 2.6 fill.3.refs_2_
  236.2 20.5 %collective-permute-done.28.refs_1_ = bf16[512,1024]{1,0:T(8,128)(2,1)} collective-permute-done((bf16[512,1024]{1,0:T(8,128)(2,1)S(1)}, bf16[512,1024]{1,0:T(8,128)(2,1)}, u32[]{:S(2)}, u32[]{:S(2)}) %collective-permute-start.28) | collective-permute-done | bytes 1048608 | tf_op jit(solution)/shard_map/ppermute | solution.py:31
  256.7 2.2 fill.4.refs_2_
  258.9 1.0 copy-done.9
  259.9 2.2 fill.5
  (53 shorter events, 0.1 us)
Async XLA Ops:
  0.6 12.1 %copy-start.6 = (bf16[512,2048]{1,0:T(8,128)(2,1)S(1)}, bf16[512,2048]{1,0:T(8,128)(2,1)}, u32[]{:S(2)}) copy-start(bf16[512,2048]{1,0:T(8,128)(2,1)} %param.5) | copy-start | bytes 6291460
  0.6 19.0 %copy-start.16 = (f32[2048]{0:T(1024)S(1)}, f32[2048]{0:T(1024)}, u32[]{:S(2)}) copy-start(f32[2048]{0:T(1024)} %param.6) | copy-start | bytes 24580
  3.4 9.9 %copy-start.18 = (bf16[2,2,128,256]{3,2,1,0:T(8,128)(2,1)S(1)}, bf16[2,2,128,256]{3,2,1,0:T(8,128)(2,1)}, u32[]{:S(2)}) copy-start(bf16[2,2,128,256]{3,2,1,0:T(8,128)(2,1)} %get-tuple-element.33) | copy-start | bytes 786436
  3.4 16.2 %copy-start.17 = (bf16[2,2,128,256]{3,2,1,0:T(8,128)(2,1)S(1)}, bf16[2,2,128,256]{3,2,1,0:T(8,128)(2,1)}, u32[]{:S(2)}) copy-start(bf16[2,2,128,256]{3,2,1,0:T(8,128)(2,1)} %get-tuple-element.34) | copy-start | bytes 786436
  3.4 9.8 %collective-permute-start = (bf16[2,2,128,256]{3,2,1,0:T(8,128)(2,1)}, bf16[2,2,128,256]{3,2,1,0:T(8,128)(2,1)S(1)}, u32[]{:S(2)}, u32[]{:S(2)}) collective-permute-start(bf16[2,2,128,256]{3,2,1,0:T(8,128)(2,1)} %get-tuple-element.28), channel_id=1, source_target_pairs={{0,16},{1,17},{2,18},{3,19},{4,20},{5,21},{6,22},{7,23},{8,24},{9,... | collective-permute-start | bytes 786440 | tf_op jit(solution)/shard_map/ppermute | solution.py:31
  5.6 14.0 %collective-permute-start.1 = (bf16[2,2,128,256]{3,2,1,0:T(8,128)(2,1)}, bf16[2,2,128,256]{3,2,1,0:T(8,128)(2,1)S(1)}, u32[]{:S(2)}, u32[]{:S(2)}) collective-permute-start(bf16[2,2,128,256]{3,2,1,0:T(8,128)(2,1)} %get-tuple-element.29), channel_id=1, source_target_pairs={{0,32},{1,33},{2,34},{3,35},{4,36},{5,37},{6,38},{7,39},{8,40},{9,... | collective-permute-start | bytes 786440 | tf_op jit(solution)/shard_map/ppermute | solution.py:31
  7.2 14.3 %collective-permute-start.2 = (bf16[2,2,128,256]{3,2,1,0:T(8,128)(2,1)}, bf16[2,2,128,256]{3,2,1,0:T(8,128)(2,1)S(1)}, u32[]{:S(2)}, u32[]{:S(2)}) collective-permute-start(bf16[2,2,128,256]{3,2,1,0:T(8,128)(2,1)} %get-tuple-element.30), channel_id=1, source_target_pairs={{0,48},{1,49},{2,50},{3,51},{4,52},{5,53},{6,54},{7,55},{8,56},{9,... | collective-permute-start | bytes 786440 | tf_op jit(solution)/shard_map/ppermute | solution.py:31
  8.8 24.4 %collective-permute-start.3 = (bf16[2,2,128,256]{3,2,1,0:T(8,128)(2,1)}, bf16[2,2,128,256]{3,2,1,0:T(8,128)(2,1)S(1)}, u32[]{:S(2)}, u32[]{:S(2)}) collective-permute-start(bf16[2,2,128,256]{3,2,1,0:T(8,128)(2,1)} %get-tuple-element.31), channel_id=1, source_target_pairs={{0,64},{1,65},{2,66},{3,67},{4,68},{5,69},{6,70},{7,71},{8,72},{9,... | collective-permute-start | bytes 786440 | tf_op jit(solution)/shard_map/ppermute | solution.py:31
  10.6 22.6 %collective-permute-start.4 = (bf16[2,2,128,256]{3,2,1,0:T(8,128)(2,1)}, bf16[2,2,128,256]{3,2,1,0:T(8,128)(2,1)S(1)}, u32[]{:S(2)}, u32[]{:S(2)}) collective-permute-start(bf16[2,2,128,256]{3,2,1,0:T(8,128)(2,1)} %get-tuple-element.32), channel_id=1, source_target_pairs={{0,80},{1,81},{2,82},{3,83},{4,84},{5,85},{6,86},{7,87},{8,88},{9,... | collective-permute-start | bytes 786440 | tf_op jit(solution)/shard_map/ppermute | solution.py:31
  13.3 8.3 %copy-start.11 = (bf16[2,2,128,256]{3,2,1,0:T(8,128)(2,1)}, bf16[2,2,128,256]{3,2,1,0:T(8,128)(2,1)S(1)}, u32[]{:S(2)}) copy-start(bf16[2,2,128,256]{3,2,1,0:T(8,128)(2,1)S(1)} %collective-permute-done.refs_1_) | copy-start | bytes 786436
  13.3 19.9 %collective-permute-start.5 = (bf16[2,2,128,256]{3,2,1,0:T(8,128)(2,1)S(1)}, bf16[2,2,128,256]{3,2,1,0:T(8,128)(2,1)}, u32[]{:S(2)}, u32[]{:S(2)}) collective-permute-start(bf16[2,2,128,256]{3,2,1,0:T(8,128)(2,1)S(1)} %copy-done.18), channel_id=1, source_target_pairs={{0,96},{1,97},{2,98},{3,99},{4,100},{5,101},{6,102},{7,103},{8,104... | collective-permute-start | bytes 786440 | tf_op jit(solution)/shard_map/ppermute | solution.py:31
  19.6 1.9 copy-start.12
  19.6 13.5 %collective-permute-start.6 = (bf16[2,2,128,256]{3,2,1,0:T(8,128)(2,1)S(1)}, bf16[2,2,128,256]{3,2,1,0:T(8,128)(2,1)}, u32[]{:S(2)}, u32[]{:S(2)}) collective-permute-start(bf16[2,2,128,256]{3,2,1,0:T(8,128)(2,1)S(1)} %copy-done.17), channel_id=1, source_target_pairs={{0,112},{1,113},{2,114},{3,115},{4,116},{5,117},{6,118},{7,119},{8... | collective-permute-start | bytes 786440 | tf_op jit(solution)/shard_map/ppermute | solution.py:31
  21.5 11.6 %copy-start.13 = (bf16[2,2,128,256]{3,2,1,0:T(8,128)(2,1)}, bf16[2,2,128,256]{3,2,1,0:T(8,128)(2,1)S(1)}, u32[]{:S(2)}) copy-start(bf16[2,2,128,256]{3,2,1,0:T(8,128)(2,1)S(1)} %collective-permute-done.2.refs_3_) | copy-start | bytes 786436
  33.1 0.7 copy-start.14
  33.1 0.8 copy-start.15
  37.0 32.1 %copy-start.10 = (bf16[2,2,128,256]{3,2,1,0:T(8,128)(2,1)S(1)}, bf16[2,2,128,256]{3,2,1,0:T(8,128)(2,1)}, u32[]{:S(2)}) copy-start(bf16[2,2,128,256]{3,2,1,0:T(8,128)(2,1)} %get-tuple-element.38) | copy-start | bytes 786436
  37.0 3.1 %collective-permute-start.7 = (bf16[128,512]{1,0:T(8,128)(2,1)}, bf16[128,512]{1,0:T(8,128)(2,1)S(1)}, u32[]{:S(2)}, u32[]{:S(2)}) collective-permute-start(bf16[128,512]{1,0:T(8,128)(2,1)} %get-tuple-element.37), channel_id=1, source_target_pairs={{0,1},{1,0},{2,3},{3,2},{4,5},{5,4},{6,7},{7,6},{8,9},{9,8},{10,11... | collective-permute-start | bytes 393224 | tf_op jit(solution)/shard_map/ppermute | solution.py:31
  41.0 13.1 %collective-permute-start.9 = (bf16[2,128,512]{2,1,0:T(8,128)(2,1)S(1)}, bf16[2,128,512]{2,1,0:T(8,128)(2,1)S(1)}, u32[]{:S(2)}, u32[]{:S(2)}) collective-permute-start(bf16[2,128,512]{2,1,0:T(8,128)(2,1)S(1)} %get-tuple-element.50), channel_id=1, source_target_pairs={{0,64},{1,65},{2,66},{3,67},{4,68},{5,69},{6,70},{7,71},{8,72},{9,... | collective-permute-start | bytes 786440 | tf_op jit(solution)/shard_map/ppermute | solution.py:31
  54.1 8.1 %collective-permute-start.12 = (bf16[2,128,512]{2,1,0:T(8,128)(2,1)S(1)}, bf16[2,128,512]{2,1,0:T(8,128)(2,1)S(1)}, u32[]{:S(2)}, u32[]{:S(2)}) collective-permute-start(bf16[2,128,512]{2,1,0:T(8,128)(2,1)S(1)} %collective-permute-done.9), channel_id=1, source_target_pairs={{0,2},{1,3},{2,4},{3,5},{4,6},{5,7},{6,0},{7,1},{8,10},{9,11},{10,... | collective-permute-start | bytes 786440 | tf_op jit(solution)/shard_map/ppermute | solution.py:31
  55.3 13.5 %collective-permute-start.11 = (bf16[2,128,512]{2,1,0:T(8,128)(2,1)S(1)}, bf16[2,128,512]{2,1,0:T(8,128)(2,1)S(1)}, u32[]{:S(2)}, u32[]{:S(2)}) collective-permute-start(bf16[2,128,512]{2,1,0:T(8,128)(2,1)S(1)} %collective-permute-done.9), channel_id=1, source_target_pairs={{0,4},{1,5},{2,6},{3,7},{4,0},{5,1},{6,2},{7,3},{8,12},{9,13},{10,... | collective-permute-start | bytes 786440 | tf_op jit(solution)/shard_map/ppermute | solution.py:31
  57.8 11.1 %collective-permute-start.10 = (bf16[2,128,512]{2,1,0:T(8,128)(2,1)S(1)}, bf16[2,128,512]{2,1,0:T(8,128)(2,1)S(1)}, u32[]{:S(2)}, u32[]{:S(2)}) collective-permute-start(bf16[2,128,512]{2,1,0:T(8,128)(2,1)S(1)} %collective-permute-done.9), channel_id=1, source_target_pairs={{0,6},{1,7},{2,0},{3,1},{4,2},{5,3},{6,4},{7,5},{8,14},{9,15},{10,... | collective-permute-start | bytes 786440 | tf_op jit(solution)/shard_map/ppermute | solution.py:31
  69.0 82.3 %copy-start = (bf16[4,2,128,512]{3,2,1,0:T(8,128)(2,1)}, bf16[4,2,128,512]{3,2,1,0:T(8,128)(2,1)S(1)}, u32[]{:S(2)}) copy-start(bf16[4,2,128,512]{3,2,1,0:T(8,128)(2,1)S(1)} %pad_maximum_fusion.1.refs_6_.refs_7_) | copy-start | bytes 3145732
  69.0 64.2 %collective-permute-start.16 = (bf16[512,2048]{1,0:T(8,128)(2,1)}, bf16[512,2048]{1,0:T(8,128)(2,1)}, u32[]{:S(2)}, u32[]{:S(2)}) collective-permute-start(bf16[512,2048]{1,0:T(8,128)(2,1)} %fusion.2.refs_2_), channel_id=1, source_target_pairs={{0,96},{1,33},{2,98},{3,35},{4,100},{5,37},{6,102},{7,39},{8,104},... | collective-permute-start | bytes 6291464 | tf_op jit(solution)/shard_map/ppermute | solution.py:31
  69.1 6.1 %collective-permute-start.8 = (bf16[2,2,128,256]{3,2,1,0:T(8,128)(2,1)S(1)}, bf16[2,2,128,256]{3,2,1,0:T(8,128)(2,1)S(1)}, u32[]{:S(2)}, u32[]{:S(2)}) collective-permute-start(bf16[2,2,128,256]{3,2,1,0:T(8,128)(2,1)S(1)} %copy-done.10), channel_id=1, source_target_pairs={{0,16},{1,17},{2,18},{3,19},{4,20},{5,21},{6,22},{7,23},{8,24},{9,... | collective-permute-start | bytes 786440 | tf_op jit(solution)/shard_map/ppermute | solution.py:31
  69.7 9.0 %collective-permute-start.20 = (bf16[2,128,512]{2,1,0:T(8,128)(2,1)S(1)}, bf16[2,128,512]{2,1,0:T(8,128)(2,1)S(1)}, u32[]{:S(2)}, u32[]{:S(2)}) collective-permute-start(bf16[2,128,512]{2,1,0:T(8,128)(2,1)S(1)} %get-tuple-element.50), channel_id=1, source_target_pairs={{0,16},{1,17},{2,18},{3,19},{4,20},{5,21},{6,22},{7,23},{8,24},{9,... | collective-permute-start | bytes 786440 | tf_op jit(solution)/shard_map/ppermute | solution.py:31
  70.6 16.7 %collective-permute-start.19 = (bf16[2,128,512]{2,1,0:T(8,128)(2,1)S(1)}, bf16[2,128,512]{2,1,0:T(8,128)(2,1)S(1)}, u32[]{:S(2)}, u32[]{:S(2)}) collective-permute-start(bf16[2,128,512]{2,1,0:T(8,128)(2,1)S(1)} %get-tuple-element.50), channel_id=1, source_target_pairs={{0,8},{1,9},{2,10},{3,11},{4,12},{5,13},{6,14},{7,15},{8,0},{9,1},... | collective-permute-start | bytes 786440 | tf_op jit(solution)/shard_map/ppermute | solution.py:31
  75.3 43.0 %collective-permute-start.15 = (bf16[2,2,2,128,256]{4,3,2,1,0:T(8,128)(2,1)S(1)}, bf16[2,2,2,128,256]{4,3,2,1,0:T(8,128)(2,1)S(1)}, u32[]{:S(2)}, u32[]{:S(2)}) collective-permute-start(bf16[2,2,2,128,256]{4,3,2,1,0:T(8,128)(2,1)S(1)} %pad_maximum_fusion.3), channel_id=1, source_target_pairs={{0,32},{1,33},{2,34},{3,35},{4,36},{5,37},{6,38},{7,39},{8,40},{9,... | collective-permute-start | bytes 1572872 | tf_op jit(solution)/shard_map/ppermute | solution.py:31
  77.8 42.2 %collective-permute-start.14 = (bf16[2,2,2,128,256]{4,3,2,1,0:T(8,128)(2,1)S(1)}, bf16[2,2,2,128,256]{4,3,2,1,0:T(8,128)(2,1)S(1)}, u32[]{:S(2)}, u32[]{:S(2)}) collective-permute-start(bf16[2,2,2,128,256]{4,3,2,1,0:T(8,128)(2,1)S(1)} %pad_maximum_fusion.3), channel_id=1, source_target_pairs={{0,64},{1,65},{2,66},{3,67},{4,68},{5,69},{6,70},{7,71},{8,72},{9,... | collective-permute-start | bytes 1572872 | tf_op jit(solution)/shard_map/ppermute | solution.py:31
  78.7 43.3 %collective-permute-start.13 = (bf16[2,2,2,128,256]{4,3,2,1,0:T(8,128)(2,1)S(1)}, bf16[2,2,2,128,256]{4,3,2,1,0:T(8,128)(2,1)S(1)}, u32[]{:S(2)}, u32[]{:S(2)}) collective-permute-start(bf16[2,2,2,128,256]{4,3,2,1,0:T(8,128)(2,1)S(1)} %pad_maximum_fusion.3), channel_id=1, source_target_pairs={{0,96},{1,97},{2,98},{3,99},{4,100},{5,101},{6,102},{7,103},{8,104... | collective-permute-start | bytes 1572872 | tf_op jit(solution)/shard_map/ppermute | solution.py:31
  87.3 5.6 %collective-permute-start.18 = (bf16[2,128,512]{2,1,0:T(8,128)(2,1)S(1)}, bf16[2,128,512]{2,1,0:T(8,128)(2,1)S(1)}, u32[]{:S(2)}, u32[]{:S(2)}) collective-permute-start(bf16[2,128,512]{2,1,0:T(8,128)(2,1)S(1)} %get-tuple-element.50), channel_id=1, source_target_pairs={{0,24},{1,25},{2,26},{3,27},{4,28},{5,29},{6,30},{7,31},{8,16},{9,... | collective-permute-start | bytes 786440 | tf_op jit(solution)/shard_map/ppermute | solution.py:31
  93.1 30.5 %copy-start.1 = (bf16[4,2,128,512]{3,2,1,0:T(8,128)(2,1)}, bf16[4,2,128,512]{3,2,1,0:T(8,128)(2,1)S(1)}, u32[]{:S(2)}) copy-start(bf16[4,2,128,512]{3,2,1,0:T(8,128)(2,1)S(1)} %pad_maximum_fusion.2.refs_2_.refs_3_) | copy-start | bytes 3145732
  93.1 40.7 %collective-permute-start.21 = (bf16[4,2,128,512]{3,2,1,0:T(8,128)(2,1)S(1)}, bf16[4,2,128,512]{3,2,1,0:T(8,128)(2,1)S(1)}, u32[]{:S(2)}, u32[]{:S(2)}) collective-permute-start(bf16[4,2,128,512]{3,2,1,0:T(8,128)(2,1)S(1)} %pad_maximum_fusion.2.refs_2_.refs_3_), channel_id=1, source_target_pairs={{0,6},{1,7},{2,0},{3,1},{4,2},{5,3},{6,4},{7,5},{8,14},{9,15},{10,... | collective-permute-start | bytes 3145736 | tf_op jit(solution)/shard_map/ppermute | solution.py:31
  118.2 21.8 %collective-permute-start.22 = (bf16[4,2,128,512]{3,2,1,0:T(8,128)(2,1)S(1)}, bf16[4,2,128,512]{3,2,1,0:T(8,128)(2,1)}, u32[]{:S(2)}, u32[]{:S(2)}) collective-permute-start(bf16[4,2,128,512]{3,2,1,0:T(8,128)(2,1)S(1)} %pad_maximum_fusion.2.refs_2_.refs_3_), channel_id=1, source_target_pairs={{0,4},{1,5},{2,6},{3,7},{4,0},{5,1},{6,2},{7,3},{8,12},{9,13},{10,... | collective-permute-start | bytes 3145736 | tf_op jit(solution)/shard_map/ppermute | solution.py:31
  120.0 31.3 %collective-permute-start.23 = (bf16[4,2,128,512]{3,2,1,0:T(8,128)(2,1)S(1)}, bf16[4,2,128,512]{3,2,1,0:T(8,128)(2,1)}, u32[]{:S(2)}, u32[]{:S(2)}) collective-permute-start(bf16[4,2,128,512]{3,2,1,0:T(8,128)(2,1)S(1)} %pad_maximum_fusion.2.refs_2_.refs_3_), channel_id=1, source_target_pairs={{0,2},{1,3},{2,4},{3,5},{4,6},{5,7},{6,0},{7,1},{8,10},{9,11},{10,... | collective-permute-start | bytes 3145736 | tf_op jit(solution)/shard_map/ppermute | solution.py:31
  133.2 66.9 %collective-permute-start.17 = (bf16[512,2048]{1,0:T(8,128)(2,1)}, bf16[512,2048]{1,0:T(8,128)(2,1)}, u32[]{:S(2)}, u32[]{:S(2)}) collective-permute-start(bf16[512,2048]{1,0:T(8,128)(2,1)} %collective-permute-done.16.refs_1_), channel_id=1, source_target_pairs={{0,1},{1,0},{2,3},{3,2},{4,5},{5,4},{6,7},{7,6},{8,9},{9,8},{10,11... | collective-permute-start | bytes 6291464 | tf_op jit(solution)/shard_map/ppermute | solution.py:31
  133.3 76.9 %collective-permute-start.29 = (bf16[512,2048]{1,0:T(8,128)(2,1)}, bf16[512,2048]{1,0:T(8,128)(2,1)}, u32[]{:S(2)}, u32[]{:S(2)}) collective-permute-start(bf16[512,2048]{1,0:T(8,128)(2,1)} %fusion.2.refs_2_), channel_id=1, source_target_pairs={{0,1},{1,0},{2,3},{3,2},{4,5},{5,4},{6,7},{7,6},{8,9},{9,8},{10,11... | collective-permute-start | bytes 6291464 | tf_op jit(solution)/shard_map/ppermute | solution.py:31
  133.8 55.3 %copy-start.2 = (bf16[4,2,128,512]{3,2,1,0:T(8,128)(2,1)}, bf16[4,2,128,512]{3,2,1,0:T(8,128)(2,1)S(1)}, u32[]{:S(2)}) copy-start(bf16[4,2,128,512]{3,2,1,0:T(8,128)(2,1)S(1)} %collective-permute-done.21.refs_3_.refs_4_) | copy-start | bytes 3145732
  133.8 17.5 %collective-permute-start.24 = (bf16[4,2,128,512]{3,2,1,0:T(8,128)(2,1)S(1)}, bf16[4,2,128,512]{3,2,1,0:T(8,128)(2,1)S(1)}, u32[]{:S(2)}, u32[]{:S(2)}) collective-permute-start(bf16[4,2,128,512]{3,2,1,0:T(8,128)(2,1)S(1)} %pad_maximum_fusion.1.refs_6_.refs_7_), channel_id=1, source_target_pairs={{0,24},{1,25},{2,26},{3,27},{4,28},{5,29},{6,30},{7,31},{8,16},{9,... | collective-permute-start | bytes 3145736 | tf_op jit(solution)/shard_map/ppermute | solution.py:31
  140.0 19.9 %collective-permute-start.25 = (bf16[4,2,128,512]{3,2,1,0:T(8,128)(2,1)S(1)}, bf16[4,2,128,512]{3,2,1,0:T(8,128)(2,1)S(1)}, u32[]{:S(2)}, u32[]{:S(2)}) collective-permute-start(bf16[4,2,128,512]{3,2,1,0:T(8,128)(2,1)S(1)} %pad_maximum_fusion.1.refs_6_.refs_7_), channel_id=1, source_target_pairs={{0,8},{1,9},{2,10},{3,11},{4,12},{5,13},{6,14},{7,15},{8,0},{9,1},... | collective-permute-start | bytes 3145736 | tf_op jit(solution)/shard_map/ppermute | solution.py:31
  151.3 37.8 %collective-permute-start.26 = (bf16[4,2,128,512]{3,2,1,0:T(8,128)(2,1)S(1)}, bf16[4,2,128,512]{3,2,1,0:T(8,128)(2,1)S(1)}, u32[]{:S(2)}, u32[]{:S(2)}) collective-permute-start(bf16[4,2,128,512]{3,2,1,0:T(8,128)(2,1)S(1)} %pad_maximum_fusion.1.refs_6_.refs_7_), channel_id=1, source_target_pairs={{0,16},{1,17},{2,18},{3,19},{4,20},{5,21},{6,22},{7,23},{8,24},{9,... | collective-permute-start | bytes 3145736 | tf_op jit(solution)/shard_map/ppermute | solution.py:31
  151.3 8.6 %copy-start.3 = (bf16[4,2,128,512]{3,2,1,0:T(8,128)(2,1)}, bf16[4,2,128,512]{3,2,1,0:T(8,128)(2,1)S(1)}, u32[]{:S(2)}) copy-start(bf16[4,2,128,512]{3,2,1,0:T(8,128)(2,1)S(1)} %collective-permute-done.24.refs_7_.refs_8_) | copy-start | bytes 3145732
  159.9 1.0 copy-start.4
  189.1 1.0 copy-start.5
  210.2 15.9 %copy-start.8 = (bf16[512,1024]{1,0:T(8,128)(2,1)S(1)}, bf16[512,1024]{1,0:T(8,128)(2,1)}, u32[]{:S(2)}) copy-start(bf16[512,1024]{1,0:T(8,128)(2,1)} %project.3) | copy-start | bytes 3145732
  210.2 15.9 %copy-start.7 = (bf16[512,1024]{1,0:T(8,128)(2,1)S(1)}, bf16[512,1024]{1,0:T(8,128)(2,1)}, u32[]{:S(2)}) copy-start(bf16[512,1024]{1,0:T(8,128)(2,1)} %project.4) | copy-start | bytes 3145732
  225.6 8.0 %collective-permute-start.30 = (bf16[512,1024]{1,0:T(8,128)(2,1)}, bf16[512,1024]{1,0:T(8,128)(2,1)}, u32[]{:S(2)}, u32[]{:S(2)}) collective-permute-start(bf16[512,1024]{1,0:T(8,128)(2,1)} %get-tuple-element.48), channel_id=1, source_target_pairs={{0,1},{1,0},{2,3},{3,2},{4,5},{5,4},{6,7},{7,6},{8,9},{9,8},{10,11... | collective-permute-start | bytes 3145736 | tf_op jit(solution)/shard_map/ppermute | solution.py:31
  226.1 30.6 %collective-permute-start.28 = (bf16[512,1024]{1,0:T(8,128)(2,1)S(1)}, bf16[512,1024]{1,0:T(8,128)(2,1)}, u32[]{:S(2)}, u32[]{:S(2)}) collective-permute-start(bf16[512,1024]{1,0:T(8,128)(2,1)S(1)} %copy-done.8), channel_id=1, source_target_pairs={{0,32},{1,97},{2,34},{3,99},{4,36},{5,101},{6,38},{7,103},{8,40},{... | collective-permute-start | bytes 3145736 | tf_op jit(solution)/shard_map/ppermute | solution.py:31
  226.1 32.8 %collective-permute-start.27 = (bf16[512,1024]{1,0:T(8,128)(2,1)S(1)}, bf16[512,1024]{1,0:T(8,128)(2,1)S(1)}, u32[]{:S(2)}, u32[]{:S(2)}) collective-permute-start(bf16[512,1024]{1,0:T(8,128)(2,1)S(1)} %copy-done.7), channel_id=1, source_target_pairs={{0,97},{1,32},{2,99},{3,34},{4,101},{5,36},{6,103},{7,38},{8,105},... | collective-permute-start | bytes 3145736 | tf_op jit(solution)/shard_map/ppermute | solution.py:31
  258.9 1.0 copy-start.9
